TPU v7x, 512 devices: a whole 4x8x8 slice. The times are simulated.
512 devices in a mesh: leaf: 128 (over y, z, core), top: 4 (over x).
Axes of the slice: x: 4, y: 8, z: 8, core: 2. Of those that a mesh axis runs over, the one named last changes fastest.
Arguments:
- charges: float32 [4, 16, 65536], P('top', None, 'leaf'), may hold values from -6 to 6
- leaf_basis: float32 [4, 1024, 64, 64], P('top', 'leaf'), may hold values from -0.75 to 0.75
- near_blocks: float32 [4, 1024, 3, 64, 64], P('top', 'leaf'), may hold values from -0.4375 to 0.4375
- near_list: int32 [4, 1024, 3], P('top', 'leaf'), may hold values from 0 to 8
- local_transfer: float32 [4, 1792, 64, 64], P('top', 'leaf'), may hold values from -0.5 to 0.5
- local_coupling: float32 [4, 1792, 3, 64, 64], P('top', 'leaf'), may hold values from -0.4375 to 0.4375
- coupling_list: int32 [4, 1792, 3], P('top', 'leaf'), may hold values from 0 to 23, as said below
- coarse_transfer: float32 [4, 7, 2, 64, 64], P('top'), may hold values from -0.5 to 0.5
- coarse_coupling: float32 [4, 5, 4, 64, 64], P('top'), may hold values from -0.4375 to 0.4375
- opposite_coupling: float32 [4, 64, 64], P('top'), may hold values from -0.75 to 0.75
- body_coupling: float32 [4, 3, 64, 64], P('top'), may hold values from -0.4375 to 0.4375
Outputs:
- potential: float32 [4, 16, 65536], P('top', None, 'leaf')
Inputs may be any that keep to these rules, and one draw needn't show every extreme that they name: `coupling_list`: for a node of a device tier with m nodes per device the entry lies below 3 m; it names, in order, the m nodes of that tier on the previous device along the boundary, then this device's, then the next device's.
All inputs are finite; a program needn't handle non-finite values.
Results may differ from a plain program's by a relative error of at most 0.0001.
Values sent between devices are 32-bit elements; how exact they have to be, the bound alone decides.
A program may use at most 64 MiB of HBM per device.

v0:
```python
import functools

import jax
import jax.numpy as jnp
from jax import lax
from jax.experimental import pallas as pl
from jax.experimental.pallas import tpu as pltpu
from jax.sharding import PartitionSpec as P

HIGH = lax.Precision.HIGH
MESH = pl.DeviceIdType.MESH
F32 = jnp.float32
K = 64
RHS = 16
NEAR = 4
L0 = 8
NODES = 14
FIRST = (0, 8, 12)


def mm(x, w):
    return lax.dot_general(x, w, (((1,), (0,)), ((), ())), precision=HIGH, preferred_element_type=F32)


def mm_t(x, w):
    return lax.dot_general(x, w, (((1,), (1,)), ((), ())), precision=HIGH, preferred_element_type=F32)


def bmm(x, w):
    return lax.dot_general(x, w, (((2,), (1,)), ((0,), (0,))), precision=HIGH, preferred_element_type=F32)


def bmm_t(x, w):
    return lax.dot_general(x, w, (((2,), (2,)), ((0,), (0,))), precision=HIGH, preferred_element_type=F32)


def pack(x):
    h = RHS // 2
    if x.ndim == 2:
        return jnp.concatenate([x[:h], x[h:]], axis=1)
    return jnp.concatenate([x[:, :h], x[:, h:]], axis=2)


def unpack(x):
    if x.ndim == 2:
        return jnp.concatenate([x[:, :K], x[:, K:]], axis=0)
    return jnp.concatenate([x[:, :, :K], x[:, :, K:]], axis=1)


def kernel(
    Y, Z, X,
    near_list_hbm, coupling_list_hbm,
    charges_hbm, basis_hbm, near_hbm, transfer_hbm, coupling_hbm,
    ct_hbm, cc_hbm, opp_hbm, bc_hbm,
    out_ref,
    charges, basis, near, transfer, coupling, ct, cc, opp, bc, near_list, coupling_list, path_mats,
    qbuf, rows, u4buf, xsrc, xbuf, gbuf, sbuf, tiers, leaves, pg_hi, pg_lo, acc,
    load_sem, ready_sem, send_sem, recv_sem,
):
    ZL = Z.bit_length() - 1
    YL = Y.bit_length() - 1
    R = ZL + 1
    COARSE = R + YL
    W = 2 * Z
    N = Y * W
    START = [2 * W - (2 * W >> c) for c in range(R)]
    TILES = 2 * W - 2

    i = lax.axis_index("leaf")
    b = lax.axis_index("top")
    k = i % 2
    z = (i // 2) % Z
    y = i // W
    j = i % W
    side = [(i // (1 << c)) % 2 for c in range(COARSE)]

    def dev(leaf, top):
        return {"leaf": leaf, "top": top}

    order = []
    for a in range(Z // 2, 0, -1):
        order.append(a)
        if Z - a != a:
            order.append(Z - a)
    order_y = []
    for a in range(Y // 2, 0, -1):
        order_y.append(a)
        if Y - a != a:
            order_y.append(Y - a)
    order_x = sorted(range(1, X), key=lambda a: -min(a, X - a))
    near_first = lambda count: sorted(range(count), key=lambda a: min(a, count - a))
    order_xy = [(x, r) for r in near_first(Y) for x in near_first(X)]
    order_xy.sort(key=lambda t: min(t[0], X - t[0]) + min(t[1], Y - t[1]))
    row_offsets = [(dz, dk) for dz in order for dk in (0, 1)] + [(0, 1)]

    def row_dev(dz, dk):
        return dev(y * W + ((z + dz) % Z) * 2 + (k + dk) % 2, b)

    def y_dev(dy):
        return dev(((y + dy) % Y) * W + j, b)

    def x_dev(dx):
        return dev(i, (b + dx) % X)

    nxt = dev((i + 1) % N, b)
    prv = dev((i + N - 1) % N, b)

    early = [(charges_hbm, charges), (basis_hbm, basis), (transfer_hbm, transfer)]
    early += [(ct_hbm.at[0, c, side[c]], path_mats.at[c]) for c in range(R)]
    later = [
        (ct_hbm, ct), (bc_hbm, bc), (opp_hbm, opp), (cc_hbm, cc), (near_hbm, near), (coupling_hbm, coupling),
        (near_list_hbm, near_list), (coupling_list_hbm, coupling_list),
    ]
    loads = [pltpu.make_async_copy(src, dst, load_sem.at[n]) for n, (src, dst) in enumerate(early + later)]
    early, later = loads[:len(early)], loads[len(early):]
    for load in early:
        load.start()

    def await_all(sem, ref):
        pltpu.make_async_copy(ref, ref, sem).wait()

    barrier = pltpu.get_barrier_semaphore()
    partners = [(min(dz, Z - dz), row_dev(dz, dk)) for dz, dk in row_offsets] + [(min(a, Y - a), y_dev(a)) for a in order_y]
    partners += [(min(a, X - a), x_dev(a)) for a in order_x] + [(1, nxt), (1, prv)]
    partners = [p for _, p in sorted(partners, key=lambda t: -t[0])]
    for p in partners:
        pl.semaphore_signal(barrier, inc=1, device_id=p, device_id_type=MESH)

    for load in early[:2]:
        load.wait()

    dens = charges[0]
    blocks = jnp.stack([dens[:, K * l:K * (l + 1)] for l in range(L0)], axis=0)
    leaves[NEAR:NEAR + L0] = pack(blocks)
    c0 = bmm(blocks, basis[0])
    for load in early[2:]:
        load.wait()
    for load in later:
        load.start()
    parts = [path_mats[c] for c in range(R)]
    while len(parts) > 1:
        parts = [mm(*parts[n:n + 2]) if n + 1 < len(parts) else parts[n] for n in range(0, len(parts), 2)]
    path = parts[0]
    up = [c0]
    for h in range(2):
        m = L0 >> h
        moved = bmm(up[-1], transfer[0, FIRST[h]:FIRST[h] + m])
        moved = moved.reshape(m // 2, 2, RHS, K)
        up.append(moved[:, 0] + moved[:, 1])
    last = [transfer[0, FIRST[2] + n] for n in range(2)]
    q_own = mm(up[2][0], mm(last[0], path)) + mm(up[2][1], mm(last[1], path))
    own = mm(up[2][0], last[0]) + mm(up[2][1], last[1])

    qbuf[j] = pack(q_own)
    rows[j] = pack(own)
    tiers[NODES:NODES + L0] = pack(up[0])
    tiers[NODES + 8:NODES + 12] = pack(up[1])
    tiers[NODES + 12:NODES + 14] = pack(up[2])

    pl.semaphore_wait(barrier, len(partners))
    for a in order_x:
        pl.semaphore_signal(ready_sem, inc=1, device_id=x_dev(a), device_id_type=MESH)

    def send_to_row(ref, at):
        for to_z in near_first(Z):
            for to_k in (1, 0):
                @pl.when((z != to_z) | (k != to_k))
                def _():
                    pltpu.make_async_remote_copy(
                        src_ref=ref.at[j], dst_ref=ref.at[j], send_sem=send_sem.at[at], recv_sem=recv_sem.at[at],
                        device_id=dev(y * W + to_z * 2 + to_k, b), device_id_type=MESH).start()

    send_to_row(qbuf, 0)

    square = (K, K)
    unit = (lax.broadcasted_iota(jnp.int32, square, 0) == lax.broadcasted_iota(jnp.int32, square, 1)).astype(F32)
    down = jnp.concatenate([unit, path.T], axis=0)[None]
    for h in (2, 1, 0):
        m = L0 >> h
        down = jnp.broadcast_to(down[:, None], (m // 2, 2, 2 * K, K)).reshape(m, 2 * K, K)
        down = bmm_t(down, transfer[0, FIRST[h]:FIRST[h] + m])
    down = bmm_t(down, basis[0])
    for l in range(0, L0, 2):
        joined = jnp.concatenate([down[l], down[l + 1]], axis=1)
        hi = joined.astype(jnp.bfloat16)
        pg_hi[:, K * l:K * (l + 2)] = hi
        pg_lo[:, K * l:K * (l + 2)] = (joined - hi.astype(F32)).astype(jnp.bfloat16)

    send_to_row(rows, 1)
    for n, (src, dst, to) in enumerate((
        (leaves.at[pl.ds(L0, NEAR)], leaves.at[pl.ds(0, NEAR)], nxt),
        (leaves.at[pl.ds(NEAR, NEAR)], leaves.at[pl.ds(NEAR + L0, NEAR)], prv),
        (tiers.at[pl.ds(NODES, NODES)], tiers.at[pl.ds(0, NODES)], nxt),
        (tiers.at[pl.ds(NODES, NODES)], tiers.at[pl.ds(2 * NODES, NODES)], prv),
    )):
        at = 2 + n // 2
        copy = pltpu.make_async_remote_copy(
            src_ref=src, dst_ref=dst, send_sem=send_sem.at[at], recv_sem=recv_sem.at[at],
            device_id=to, device_id_type=MESH)
        copy.start()

    for load in later:
        load.wait()

    path_y = ct[0, R, side[R]]
    for c in range(R + 1, COARSE):
        path_y = mm(path_y, ct[0, c, side[c]])
    for s in range(X - 1):
        sbuf[s] = mm_t(bc[0, s], path_y)
    if R == COARSE - 3:
        for n in range(2):
            sbuf[X - 1 + n] = mm_t(mm(ct[0, R, n], opp[0]), ct[0, R, side[R]])


    await_all(recv_sem.at[0], qbuf.at[pl.ds(1, W - 1)])
    total = qbuf[0]
    for n in range(1, W):
        total = total + qbuf[n]
    u_row = unpack(total)
    xsrc[...] = pack(mm(u_row, path_y))
    u4buf[y] = total
    pl.semaphore_wait(ready_sem, len(order_x))
    for to_x, to_y in order_xy:
        @pl.when(b != to_x)
        def _():
            pltpu.make_async_remote_copy(
                src_ref=xsrc, dst_ref=xbuf.at[((b - to_x + X) % X) * Y + y], send_sem=send_sem.at[5],
                recv_sem=recv_sem.at[5], device_id=dev(to_y * W + j, to_x), device_id_type=MESH).start()

        @pl.when((b == to_x) & (y != to_y))
        def _():
            pltpu.make_async_remote_copy(
                src_ref=u4buf.at[y], dst_ref=u4buf.at[y], send_sem=send_sem.at[4], recv_sem=recv_sem.at[4],
                device_id=dev(to_y * W + j, b), device_id_type=MESH).start()

    await_all(recv_sem.at[1], rows.at[pl.ds(0, W - 1)])
    tier = unpack(rows[0:W])
    for c in range(R - 1):
        m = W >> c
        pairs = tier.reshape(m // 2, 2, RHS, K)
        left = mm(pairs[:, 0].reshape(m // 2 * RHS, K), ct[0, c, 0])
        right = mm(pairs[:, 1].reshape(m // 2 * RHS, K), ct[0, c, 1])
        tier = (left + right).reshape(m // 2, RHS, K)
        rows[START[c + 1]:START[c + 1] + m // 2] = pack(tier)

    given = None
    for c in range(R - 1, -1, -1):
        m = W >> c
        if given is None:
            given = [jnp.zeros((RHS, K), F32)] * 3
        else:
            moved = mm_t(jnp.concatenate(given, axis=0), ct[0, c, side[c]])
            given = [moved[RHS * n:RHS * (n + 1)] for n in range(3)]
        third = 3 - 6 * side[c]
        for offset, slot in ((-2, 1), (2, 2), (third, 3 - 3 * side[c])):
            at = j // (1 << c) + offset
            term = mm(unpack(rows[START[c] + (at + m) % m]), cc[0, c, slot])
            for n, keep in enumerate((at >= m, (at >= 0) & (at < m), at < 0)):
                given[n] = given[n] + jnp.where(keep, term, 0.0)
    v_own = given[1]
    gbuf[0] = pack(given[0])
    gbuf[1] = pack(given[2])
    for n, to in enumerate((y_dev(Y - 1), y_dev(1))):
        copy = pltpu.make_async_remote_copy(
            src_ref=gbuf.at[n], dst_ref=gbuf.at[2 + n], send_sem=send_sem.at[6], recv_sem=recv_sem.at[6],
            device_id=to, device_id_type=MESH)
        copy.start()

    await_all(recv_sem.at[2], leaves.at[pl.ds(0, 2 * NEAR)])
    for l in range(L0):
        total = None
        for s in range(3):
            term = mm(unpack(leaves[near_list[s, 0, l] + l]), near[0, l, s])
            total = term if total is None else total + term
        acc[l] = total

    await_all(recv_sem.at[3], tiers.at[pl.ds(0, 2 * NODES)])
    coupled = []
    for h in range(3):
        m = L0 >> h
        terms = []
        for n in range(m):
            node = FIRST[h] + n
            total = None
            for s in range(3):
                e = coupling_list[s, 0, node]
                where = (e // m) * NODES + FIRST[h] + e % m
                term = mm(unpack(tiers[where]), coupling[0, node, s])
                total = term if total is None else total + term
            terms.append(total)
        coupled.append(jnp.stack(terms, axis=0))

    local = coupled[2]
    for h in (1, 0):
        m = L0 >> h
        local = jnp.broadcast_to(local[:, None], (m // 2, 2, RHS, K)).reshape(m, RHS, K)
        local = coupled[h] + bmm_t(local, transfer[0, FIRST[h]:FIRST[h] + m])
    field = bmm_t(local, basis[0]) + acc[...]
    for l in range(0, L0, 2):
        out_ref[0, :, K * l:K * (l + 2)] = jnp.concatenate([field[l], field[l + 1]], axis=1)

    await_all(recv_sem.at[6], gbuf.at[pl.ds(2, 2)])
    v_own = v_own + unpack(gbuf[2]) + unpack(gbuf[3])

    await_all(recv_sem.at[4], u4buf.at[pl.ds(0, Y - 1)])
    if R == COARSE - 3:
        third = 3 - 6 * side[R]
        row = None
        for offset, slot in ((-2, 1), (2, 2), (third, 3 - 3 * side[R])):
            term = mm(unpack(u4buf[(y + offset + Y) % Y]), cc[0, R, slot])
            row = term if row is None else row + term
        pair = 2 * ((y // 2 + 2) % (Y // 2))
        row = row + mm(unpack(u4buf[pair]), sbuf[X - 1]) + mm(unpack(u4buf[pair + 1]), sbuf[X])
    else:
        row = mm(unpack(u4buf[(y + 2) % Y]), opp[0])

    await_all(recv_sem.at[5], xbuf.at[pl.ds(Y, (X - 1) * Y)])
    for s in range(X - 1):
        total = xbuf[(s + 1) * Y]
        for n in range(1, Y):
            total = total + xbuf[(s + 1) * Y + n]
        row = row + mm(unpack(total), sbuf[s])
    late = jnp.concatenate([v_own, row], axis=1)
    hi = late.astype(jnp.bfloat16)
    lo = (late - hi.astype(F32)).astype(jnp.bfloat16)
    both = jnp.dot(jnp.concatenate([hi, lo], axis=0), pg_hi[...], preferred_element_type=F32)
    out_ref[0] = out_ref[0] + (both[:RHS] + both[RHS:] + jnp.dot(hi, pg_lo[...], preferred_element_type=F32))

    await_all(send_sem.at[0], qbuf.at[pl.ds(1, W - 1)])
    await_all(send_sem.at[1], rows.at[pl.ds(0, W - 1)])
    await_all(send_sem.at[2], leaves.at[pl.ds(0, 2 * NEAR)])
    await_all(send_sem.at[3], tiers.at[pl.ds(0, 2 * NODES)])
    await_all(send_sem.at[4], u4buf.at[pl.ds(0, Y - 1)])
    await_all(send_sem.at[5], xbuf.at[pl.ds(Y, (X - 1) * Y)])
    await_all(send_sem.at[6], gbuf.at[pl.ds(2, 2)])


def per_device(Y, Z, X, charges, leaf_basis, near_blocks, near_list, local_transfer, local_coupling, coupling_list,
               coarse_transfer, coarse_coupling, opposite_coupling, body_coupling):
    near_at = near_list.transpose(2, 0, 1)
    coupling_at = coupling_list.transpose(2, 0, 1)
    W = 2 * Z
    R = Z.bit_length()
    dma = pltpu.SemaphoreType.DMA
    vm = lambda *shape: pltpu.VMEM(shape, F32)
    operands = (charges, leaf_basis, near_blocks, local_transfer, local_coupling,
                coarse_transfer, coarse_coupling, opposite_coupling, body_coupling)
    return pl.pallas_call(
        functools.partial(kernel, Y, Z, X),
        out_shape=pltpu.VMEM(charges.shape, F32),
        in_specs=[pl.BlockSpec(memory_space=pltpu.HBM)] * 11,
        out_specs=pl.BlockSpec(memory_space=pltpu.VMEM),
        scratch_shapes=[
            *[vm(*a.shape) for a in operands],
            pltpu.SMEM(near_at.shape, jnp.int32), pltpu.SMEM(coupling_at.shape, jnp.int32),
            vm(R, K, K),
            vm(W, 8, 128), vm(2 * W - 2, 8, 128), vm(Y, 8, 128), vm(8, 128), vm(X * Y, 8, 128), vm(4, 8, 128), vm(X + 1, K, K),
            vm(3 * NODES, 8, 128), vm(L0 + 2 * NEAR, 8, 128),
            pltpu.VMEM((2 * K, L0 * K), jnp.bfloat16), pltpu.VMEM((2 * K, L0 * K), jnp.bfloat16), vm(L0, RHS, K),
            dma((11 + R,)), pltpu.SemaphoreType.REGULAR, dma((7,)), dma((7,)),
        ],
        compiler_params=pltpu.CompilerParams(collective_id=0, has_side_effects=True),
    )(near_at, coupling_at, *operands)


def solution(mesh):
    n = mesh.shape["leaf"]
    Z = 8 if n == 128 else 2
    Y = n // (2 * Z)
    X = mesh.shape["top"]
    in_specs = (
        P("top", None, "leaf"),
        P("top", "leaf", None, None),
        P("top", "leaf", None, None, None),
        P("top", "leaf", None),
        P("top", "leaf", None, None),
        P("top", "leaf", None, None, None),
        P("top", "leaf", None),
        P("top", None, None, None, None),
        P("top", None, None, None, None),
        P("top", None, None),
        P("top", None, None, None),
    )
    return jax.shard_map(
        functools.partial(per_device, Y, Z, X), mesh=mesh, in_specs=in_specs,
        out_specs=P("top", None, "leaf"), check_vma=False
    )
```

profile of v0, /device:TPU:1, one launch (start us, length us, event | category | flops | bytes accessed | tf_op | source)
XLA Modules:
  0.0 27.0 jit_solution(4343939943457508785)
XLA Ops:
  0.0 26.4 %shard_map.109 = f32[1,16,512]{2,1,0:T(8,128)S(1)} custom-call(s32[3,1,8]{2,1,0:T(1,128)} %bitcast.2, s32[3,1,14]{2,1,0:T(1,128)} %bitcast.3, f32[1,16,512]{2,1,0:T(8,128)} %charges_hbm.1, f32[1,8,64,64]{3,2,1,0:T(8,128)} %basis_hbm.1, f32[1,8,3,64,64]{4,3,2,1,0:T(8,128)} %near_hbm.1, f32[1,14,64,64]{3,2,1,0:T(8,128)} %transfer_hbm.1, ...), custom_call_target="tpu_custom_call" | custom-call | tf_op jit(solution)/shard_map/pallas_call | solution.py:348
  26.4 0.6 %copy.13 = f32[1,16,512]{2,1,0:T(8,128)} copy(f32[1,16,512]{2,1,0:T(8,128)S(1)} %shard_map.109) | data formatting | bytes 65536
where the time goes:
time: 27.1 us; the launch traced here: 27 us
  Pallas kernels  26.4 us (97%)
  local copies, waits for them, and re-layouts  0.62 us (2%)
    pallas_call x1, Pallas kernels, per_device(): pl.pallas_call(functools.partial(kernel, Y, Z, X), out_shape=pltpu.VMEM(c...  26.4 us
    unnamed x1, local copies, waits for them, and re-layouts  0.62 us

commit v1 on v0

--- a/solution.py
+++ b/solution.py
@@ -18,20 +18,35 @@
 FIRST = (0, 8, 12)
 
 
+def split(a):
+    hi = a.astype(jnp.bfloat16)
+    return hi, (a - hi.astype(F32)).astype(jnp.bfloat16)
+
+
+def product(x, w, dims):
+    rows = x.ndim - 2
+    xh, xl = split(x)
+    wh, wl = w if isinstance(w, tuple) else split(w)
+    dot = functools.partial(lax.dot_general, dimension_numbers=dims, preferred_element_type=F32)
+    both = dot(jnp.concatenate([xh, xl], axis=rows), wh)
+    m = x.shape[rows]
+    return lax.slice_in_dim(both, 0, m, axis=rows) + (lax.slice_in_dim(both, m, 2 * m, axis=rows) + dot(xh, wl))
+
+
 def mm(x, w):
-    return lax.dot_general(x, w, (((1,), (0,)), ((), ())), precision=HIGH, preferred_element_type=F32)
+    return product(x, w, (((1,), (0,)), ((), ())))
 
 
 def mm_t(x, w):
-    return lax.dot_general(x, w, (((1,), (1,)), ((), ())), precision=HIGH, preferred_element_type=F32)
+    return product(x, w, (((1,), (1,)), ((), ())))
 
 
 def bmm(x, w):
-    return lax.dot_general(x, w, (((2,), (1,)), ((0,), (0,))), precision=HIGH, preferred_element_type=F32)
+    return product(x, w, (((2,), (1,)), ((0,), (0,))))
 
 
 def bmm_t(x, w):
-    return lax.dot_general(x, w, (((2,), (2,)), ((0,), (0,))), precision=HIGH, preferred_element_type=F32)
+    return product(x, w, (((2,), (2,)), ((0,), (0,))))
 
 
 def pack(x):
@@ -53,9 +68,9 @@
     charges_hbm, basis_hbm, near_hbm, transfer_hbm, coupling_hbm,
     ct_hbm, cc_hbm, opp_hbm, bc_hbm,
     out_ref,
-    charges, basis, near, transfer, coupling, ct, cc, opp, bc, near_list, coupling_list, path_mats,
-    qbuf, rows, u4buf, xsrc, xbuf, gbuf, sbuf, tiers, leaves, pg_hi, pg_lo, acc,
-    load_sem, ready_sem, send_sem, recv_sem,
+    charges, basis, near, transfer, coupling, ct, cc, opp, bc, near_list, coupling_list,
+    qbuf, rows, u4buf, xsrc, xbuf, gbuf, sbuf, tiers, leaves, pg_hi, pg_lo, far_hi, far_lo, acc,
+    vbuf, load_sem, state, send_sem, recv_sem,
 ):
     ZL = Z.bit_length() - 1
     YL = Y.bit_length() - 1
@@ -72,6 +87,12 @@
     z = (i // 2) % Z
     y = i // W
     j = i % W
+    half = Z // 2
+    first = z < half
+    second = z >= half
+    origin = (z == 0) & (k == 0)
+    final = (z == Z - 1) & (k == 1)
+    one = lambda flag: jnp.where(flag, 1, 0)
     side = [(i // (1 << c)) % 2 for c in range(COARSE)]
 
     def dev(leaf, top):
@@ -105,8 +126,7 @@
     nxt = dev((i + 1) % N, b)
     prv = dev((i + N - 1) % N, b)
 
-    early = [(charges_hbm, charges), (basis_hbm, basis), (transfer_hbm, transfer)]
-    early += [(ct_hbm.at[0, c, side[c]], path_mats.at[c]) for c in range(R)]
+    early = [(charges_hbm, charges), (basis_hbm, basis), (transfer_hbm.at[0], transfer.at[0, pl.ds(0, NODES)])]
     later = [
         (ct_hbm, ct), (bc_hbm, bc), (opp_hbm, opp), (cc_hbm, cc), (near_hbm, near), (coupling_hbm, coupling),
         (near_list_hbm, near_list), (coupling_list_hbm, coupling_list),
@@ -115,16 +135,25 @@
     early, later = loads[:len(early)], loads[len(early):]
     for load in early:
         load.start()
+    for c in range(R):
+        pltpu.make_async_copy(ct_hbm.at[0, c, side[c]], transfer.at[0, NODES + c], load_sem.at[2]).start()
 
     def await_all(sem, ref):
         pltpu.make_async_copy(ref, ref, sem).wait()
 
     barrier = pltpu.get_barrier_semaphore()
     partners = [(min(dz, Z - dz), row_dev(dz, dk)) for dz, dk in row_offsets] + [(min(a, Y - a), y_dev(a)) for a in order_y]
-    partners += [(min(a, X - a), x_dev(a)) for a in order_x] + [(1, nxt), (1, prv)]
+    partners += [(min(a, X - a), x_dev(a)) for a in order_x]
     partners = [p for _, p in sorted(partners, key=lambda t: -t[0])]
-    for p in partners:
-        pl.semaphore_signal(barrier, inc=1, device_id=p, device_id_type=MESH)
+
+    @pl.when(first)
+    def _():
+        for p in partners:
+            pl.semaphore_signal(barrier, inc=1, device_id=p, device_id_type=MESH)
+
+    @pl.when(origin)
+    def _():
+        pl.semaphore_signal(barrier, inc=1, device_id=prv, device_id_type=MESH)
 
     for load in early[:2]:
         load.wait()
@@ -133,11 +162,10 @@
     blocks = jnp.stack([dens[:, K * l:K * (l + 1)] for l in range(L0)], axis=0)
     leaves[NEAR:NEAR + L0] = pack(blocks)
     c0 = bmm(blocks, basis[0])
-    for load in early[2:]:
-        load.wait()
+    pltpu.make_async_copy(transfer, transfer, load_sem.at[2]).wait()
     for load in later:
         load.start()
-    parts = [path_mats[c] for c in range(R)]
+    parts = [transfer[0, NODES + c] for c in range(R)]
     while len(parts) > 1:
         parts = [mm(*parts[n:n + 2]) if n + 1 < len(parts) else parts[n] for n in range(0, len(parts), 2)]
     path = parts[0]
@@ -157,20 +185,36 @@
     tiers[NODES + 8:NODES + 12] = pack(up[1])
     tiers[NODES + 12:NODES + 14] = pack(up[2])
 
-    pl.semaphore_wait(barrier, len(partners))
-    for a in order_x:
-        pl.semaphore_signal(ready_sem, inc=1, device_id=x_dev(a), device_id_type=MESH)
-
-    def send_to_row(ref, at):
-        for to_z in near_first(Z):
+    pl.semaphore_wait(barrier, 2 * half + one(final) + one(first) * (len(order_y) + len(order_x) - 1))
+
+    @pl.when(first)
+    def _():
+        for a in order_x:
+            pl.semaphore_signal(state.at[0], inc=1, device_id=x_dev(a), device_id_type=MESH)
+
+    @pl.when(second)
+    def _():
+        for to_z in range(half):
+            for to_k in range(2):
+                pl.semaphore_signal(state.at[1], inc=1, device_id=dev(y * W + to_z * 2 + to_k, b), device_id_type=MESH)
+
+    @pl.when(final)
+    def _():
+        pl.semaphore_signal(state.at[1], inc=1, device_id=nxt, device_id_type=MESH)
+
+    mate = dev(y * W + (Z - 1 - z) * 2 + k, b)
+
+    def send_to_row(ref, at, places):
+        for to_z in places:
             for to_k in (1, 0):
                 @pl.when((z != to_z) | (k != to_k))
                 def _():
                     pltpu.make_async_remote_copy(
-                        src_ref=ref.at[j], dst_ref=ref.at[j], send_sem=send_sem.at[at], recv_sem=recv_sem.at[at],
+                        src_ref=ref.at[j], dst_ref=ref.at[j], send_sem=send_sem.at[0], recv_sem=recv_sem.at[at],
                         device_id=dev(y * W + to_z * 2 + to_k, b), device_id_type=MESH).start()
 
-    send_to_row(qbuf, 0)
+    places = near_first(Z)
+    send_to_row(qbuf, 0, [p for p in places if p < half])
 
     square = (K, K)
     unit = (lax.broadcasted_iota(jnp.int32, square, 0) == lax.broadcasted_iota(jnp.int32, square, 1)).astype(F32)
@@ -186,18 +230,43 @@
         pg_hi[:, K * l:K * (l + 2)] = hi
         pg_lo[:, K * l:K * (l + 2)] = (joined - hi.astype(F32)).astype(jnp.bfloat16)
 
-    send_to_row(rows, 1)
-    for n, (src, dst, to) in enumerate((
+    halo_next = (
         (leaves.at[pl.ds(L0, NEAR)], leaves.at[pl.ds(0, NEAR)], nxt),
+        (tiers.at[pl.ds(NODES, NODES)], tiers.at[pl.ds(0, NODES)], nxt),
+    )
+    halo_previous = (
         (leaves.at[pl.ds(NEAR, NEAR)], leaves.at[pl.ds(NEAR + L0, NEAR)], prv),
-        (tiers.at[pl.ds(NODES, NODES)], tiers.at[pl.ds(0, NODES)], nxt),
         (tiers.at[pl.ds(NODES, NODES)], tiers.at[pl.ds(2 * NODES, NODES)], prv),
-    )):
-        at = 2 + n // 2
-        copy = pltpu.make_async_remote_copy(
-            src_ref=src, dst_ref=dst, send_sem=send_sem.at[at], recv_sem=recv_sem.at[at],
-            device_id=to, device_id_type=MESH)
-        copy.start()
+    )
+
+    def send_halo(parts):
+        for src, dst, to in parts:
+            pltpu.make_async_remote_copy(
+                src_ref=src, dst_ref=dst, send_sem=send_sem.at[1], recv_sem=recv_sem.at[2],
+                device_id=to, device_id_type=MESH).start()
+
+    send_to_row(rows, 1, [p for p in places if p < half])
+
+    @pl.when(final)
+    def _():
+        send_halo(halo_next)
+
+    @pl.when(first)
+    def _():
+        pl.semaphore_wait(state.at[1], 2 * half + one(origin))
+        for a in (1, Y - 1):
+            pl.semaphore_signal(state.at[2], inc=1, device_id=y_dev(a), device_id_type=MESH)
+
+    @pl.when(second)
+    def _():
+        pl.semaphore_wait(state.at[3], 1)
+
+    send_to_row(rows, 1, [p for p in places if p >= half])
+    @pl.when(jnp.logical_not(final))
+    def _():
+        send_halo(halo_next)
+
+    send_halo(halo_previous)
 
     for load in later:
         load.wait()
@@ -212,26 +281,32 @@
             sbuf[X - 1 + n] = mm_t(mm(ct[0, R, n], opp[0]), ct[0, R, side[R]])
 
 
-    await_all(recv_sem.at[0], qbuf.at[pl.ds(1, W - 1)])
-    total = qbuf[0]
-    for n in range(1, W):
-        total = total + qbuf[n]
-    u_row = unpack(total)
-    xsrc[...] = pack(mm(u_row, path_y))
-    u4buf[y] = total
-    pl.semaphore_wait(ready_sem, len(order_x))
-    for to_x, to_y in order_xy:
-        @pl.when(b != to_x)
-        def _():
-            pltpu.make_async_remote_copy(
-                src_ref=xsrc, dst_ref=xbuf.at[((b - to_x + X) % X) * Y + y], send_sem=send_sem.at[5],
-                recv_sem=recv_sem.at[5], device_id=dev(to_y * W + j, to_x), device_id_type=MESH).start()
-
-        @pl.when((b == to_x) & (y != to_y))
-        def _():
-            pltpu.make_async_remote_copy(
-                src_ref=u4buf.at[y], dst_ref=u4buf.at[y], send_sem=send_sem.at[4], recv_sem=recv_sem.at[4],
-                device_id=dev(to_y * W + j, b), device_id_type=MESH).start()
+    @pl.when(first)
+    def _():
+        for s in range(X - 1):
+            far_hi[s], far_lo[s] = split(mm(sbuf[s], (pg_hi[K:], pg_lo[K:])))
+        await_all(recv_sem.at[0], qbuf.at[pl.ds(1, W - 1)])
+        total = qbuf[0]
+        for n in range(1, W):
+            total = total + qbuf[n]
+        u_row = unpack(total)
+        xsrc[...] = pack(mm(u_row, path_y))
+        u4buf[y] = total
+        pl.semaphore_wait(state.at[0], len(order_x))
+        for to_x, to_y in order_xy:
+            @pl.when(b != to_x)
+            def _():
+                pltpu.make_async_remote_copy(
+                    src_ref=xsrc, dst_ref=xbuf.at[((b - to_x + X) % X) * Y + y], send_sem=send_sem.at[2],
+                    recv_sem=recv_sem.at[5], device_id=dev(to_y * W + j, to_x), device_id_type=MESH).start()
+
+            @pl.when((b == to_x) & (y != to_y))
+            def _():
+                pltpu.make_async_remote_copy(
+                    src_ref=u4buf.at[y], dst_ref=u4buf.at[y], send_sem=send_sem.at[2], recv_sem=recv_sem.at[4],
+                    device_id=dev(to_y * W + j, b), device_id_type=MESH).start()
+        pl.semaphore_wait(state.at[2], 2)
+        pl.semaphore_signal(state.at[3], inc=1, device_id=mate, device_id_type=MESH)
 
     await_all(recv_sem.at[1], rows.at[pl.ds(0, W - 1)])
     tier = unpack(rows[0:W])
@@ -262,11 +337,11 @@
     gbuf[1] = pack(given[2])
     for n, to in enumerate((y_dev(Y - 1), y_dev(1))):
         copy = pltpu.make_async_remote_copy(
-            src_ref=gbuf.at[n], dst_ref=gbuf.at[2 + n], send_sem=send_sem.at[6], recv_sem=recv_sem.at[6],
+            src_ref=gbuf.at[n], dst_ref=gbuf.at[2 + n], send_sem=send_sem.at[1], recv_sem=recv_sem.at[3],
             device_id=to, device_id_type=MESH)
         copy.start()
 
-    await_all(recv_sem.at[2], leaves.at[pl.ds(0, 2 * NEAR)])
+    await_all(recv_sem.at[2], tiers.at[pl.ds(0, 2 * NEAR + 2 * NODES)])
     for l in range(L0):
         total = None
         for s in range(3):
@@ -274,7 +349,6 @@
             total = term if total is None else total + term
         acc[l] = total
 
-    await_all(recv_sem.at[3], tiers.at[pl.ds(0, 2 * NODES)])
     coupled = []
     for h in range(3):
         m = L0 >> h
@@ -299,40 +373,64 @@
     for l in range(0, L0, 2):
         out_ref[0, :, K * l:K * (l + 2)] = jnp.concatenate([field[l], field[l + 1]], axis=1)
 
-    await_all(recv_sem.at[6], gbuf.at[pl.ds(2, 2)])
+    await_all(recv_sem.at[3], gbuf.at[pl.ds(2, 2)])
     v_own = v_own + unpack(gbuf[2]) + unpack(gbuf[3])
 
-    await_all(recv_sem.at[4], u4buf.at[pl.ds(0, Y - 1)])
-    if R == COARSE - 3:
-        third = 3 - 6 * side[R]
-        row = None
-        for offset, slot in ((-2, 1), (2, 2), (third, 3 - 3 * side[R])):
-            term = mm(unpack(u4buf[(y + offset + Y) % Y]), cc[0, R, slot])
-            row = term if row is None else row + term
-        pair = 2 * ((y // 2 + 2) % (Y // 2))
-        row = row + mm(unpack(u4buf[pair]), sbuf[X - 1]) + mm(unpack(u4buf[pair + 1]), sbuf[X])
-    else:
-        row = mm(unpack(u4buf[(y + 2) % Y]), opp[0])
-
-    await_all(recv_sem.at[5], xbuf.at[pl.ds(Y, (X - 1) * Y)])
-    for s in range(X - 1):
-        total = xbuf[(s + 1) * Y]
-        for n in range(1, Y):
-            total = total + xbuf[(s + 1) * Y + n]
-        row = row + mm(unpack(total), sbuf[s])
-    late = jnp.concatenate([v_own, row], axis=1)
-    hi = late.astype(jnp.bfloat16)
-    lo = (late - hi.astype(F32)).astype(jnp.bfloat16)
-    both = jnp.dot(jnp.concatenate([hi, lo], axis=0), pg_hi[...], preferred_element_type=F32)
-    out_ref[0] = out_ref[0] + (both[:RHS] + both[RHS:] + jnp.dot(hi, pg_lo[...], preferred_element_type=F32))
-
-    await_all(send_sem.at[0], qbuf.at[pl.ds(1, W - 1)])
-    await_all(send_sem.at[1], rows.at[pl.ds(0, W - 1)])
-    await_all(send_sem.at[2], leaves.at[pl.ds(0, 2 * NEAR)])
-    await_all(send_sem.at[3], tiers.at[pl.ds(0, 2 * NODES)])
-    await_all(send_sem.at[4], u4buf.at[pl.ds(0, Y - 1)])
-    await_all(send_sem.at[5], xbuf.at[pl.ds(Y, (X - 1) * Y)])
-    await_all(send_sem.at[6], gbuf.at[pl.ds(2, 2)])
+    def finish(row):
+        late = mm(jnp.concatenate([v_own, row], axis=1), (pg_hi[...], pg_lo[...]))
+        out_ref[0] = out_ref[0] + late
+
+    @pl.when(first)
+    def _():
+        await_all(recv_sem.at[4], u4buf.at[pl.ds(0, Y - 1)])
+        if R == COARSE - 3:
+            third = 3 - 6 * side[R]
+            row = None
+            for offset, slot in ((-2, 1), (2, 2), (third, 3 - 3 * side[R])):
+                term = mm(unpack(u4buf[(y + offset + Y) % Y]), cc[0, R, slot])
+                row = term if row is None else row + term
+            pair = 2 * ((y // 2 + 2) % (Y // 2))
+            row = row + mm(unpack(u4buf[pair]), sbuf[X - 1]) + mm(unpack(u4buf[pair + 1]), sbuf[X])
+        else:
+            row = mm(unpack(u4buf[(y + 2) % Y]), opp[0])
+
+        finish(row)
+
+        await_all(recv_sem.at[5], xbuf.at[pl.ds(Y, (X - 1) * Y)])
+        bodies = []
+        for s in range(X - 1):
+            total = xbuf[(s + 1) * Y]
+            for n in range(1, Y):
+                total = total + xbuf[(s + 1) * Y + n]
+            bodies.append(unpack(total))
+        late = None
+        for s in range(X - 1):
+            term = mm(bodies[s], (far_hi[s], far_lo[s]))
+            late = term if late is None else late + term
+        out_ref[0] = out_ref[0] + late
+
+        @pl.when(z == half - 1)
+        def _():
+            whole = row
+            for s in range(X - 1):
+                whole = whole + mm(bodies[s], sbuf[s])
+            vbuf[...] = pack(whole)
+            for to_z in range(Z - 1, half - 1, -1):
+                pltpu.make_async_remote_copy(
+                    src_ref=vbuf, dst_ref=vbuf, send_sem=send_sem.at[3], recv_sem=recv_sem.at[6],
+                    device_id=dev(y * W + to_z * 2 + k, b), device_id_type=MESH).start()
+            await_all(send_sem.at[3], xbuf.at[pl.ds(0, Z - half)])
+
+        await_all(send_sem.at[0], xbuf.at[pl.ds(0, 2 * half - 1 + W - 1)])
+        await_all(send_sem.at[2], xbuf.at[pl.ds(0, Y - 1 + (X - 1) * Y)])
+
+    @pl.when(second)
+    def _():
+        await_all(recv_sem.at[6], vbuf)
+        finish(unpack(vbuf[...]))
+        await_all(send_sem.at[0], xbuf.at[pl.ds(0, 2 * half + W - 1)])
+
+    await_all(send_sem.at[1], tiers.at[pl.ds(0, 2 * NEAR + 2 * NODES + 2)])
 
 
 def per_device(Y, Z, X, charges, leaf_basis, near_blocks, near_list, local_transfer, local_coupling, coupling_list,
@@ -351,13 +449,12 @@
         in_specs=[pl.BlockSpec(memory_space=pltpu.HBM)] * 11,
         out_specs=pl.BlockSpec(memory_space=pltpu.VMEM),
         scratch_shapes=[
-            *[vm(*a.shape) for a in operands],
+            *[vm(*a.shape) for a in operands[:3]], vm(1, NODES + R, K, K), *[vm(*a.shape) for a in operands[4:]],
             pltpu.SMEM(near_at.shape, jnp.int32), pltpu.SMEM(coupling_at.shape, jnp.int32),
-            vm(R, K, K),
             vm(W, 8, 128), vm(2 * W - 2, 8, 128), vm(Y, 8, 128), vm(8, 128), vm(X * Y, 8, 128), vm(4, 8, 128), vm(X + 1, K, K),
             vm(3 * NODES, 8, 128), vm(L0 + 2 * NEAR, 8, 128),
-            pltpu.VMEM((2 * K, L0 * K), jnp.bfloat16), pltpu.VMEM((2 * K, L0 * K), jnp.bfloat16), vm(L0, RHS, K),
-            dma((11 + R,)), pltpu.SemaphoreType.REGULAR, dma((7,)), dma((7,)),
+            *[pltpu.VMEM((2 * K, L0 * K), jnp.bfloat16)] * 2, *[pltpu.VMEM((X - 1, K, L0 * K), jnp.bfloat16)] * 2, vm(L0, RHS, K),
+            vm(8, 128), dma((11,)), pltpu.SemaphoreType.REGULAR((4,)), dma((4,)), dma((7,)),
         ],
         compiler_params=pltpu.CompilerParams(collective_id=0, has_side_effects=True),
     )(near_at, coupling_at, *operands)

time: 27.1 us -> 27.2 us (level)
  no operation moved by 1% of the time
where the time goes in v1:
time: 27.2 us; the launch traced here: 27.1 us
  Pallas kernels  26.4 us (97%)
  local copies, waits for them, and re-layouts  0.62 us (2%)
    pallas_call x1, Pallas kernels, per_device(): pl.pallas_call(functools.partial(kernel, Y, Z, X), out_shape=pltpu.VMEM(c...  26.4 us
    unnamed x1, local copies, waits for them, and re-layouts  0.62 us

profile of v1, /device:TPU:1, one launch (start us, length us, event | category | flops | bytes accessed | tf_op | source)
XLA Modules:
  0.0 27.1 jit_solution(5777843186814295823)
XLA Ops:
  0.0 26.4 %shard_map.109 = f32[1,16,512]{2,1,0:T(8,128)S(1)} custom-call(s32[3,1,8]{2,1,0:T(1,128)} %bitcast.2, s32[3,1,14]{2,1,0:T(1,128)} %bitcast.3, f32[1,16,512]{2,1,0:T(8,128)} %charges_hbm.1, f32[1,8,64,64]{3,2,1,0:T(8,128)} %basis_hbm.1, f32[1,8,3,64,64]{4,3,2,1,0:T(8,128)} %near_hbm.1, f32[1,14,64,64]{3,2,1,0:T(8,128)} %transfer_hbm.1, ...), custom_call_target="tpu_custom_call" | custom-call | tf_op jit(solution)/shard_map/pallas_call | solution.py:446
  26.4 0.6 %copy.13 = f32[1,16,512]{2,1,0:T(8,128)} copy(f32[1,16,512]{2,1,0:T(8,128)S(1)} %shard_map.109) | data formatting | bytes 65536

commit v2 on v1

--- a/solution.py
+++ b/solution.py
@@ -230,6 +230,19 @@
         pg_hi[:, K * l:K * (l + 2)] = hi
         pg_lo[:, K * l:K * (l + 2)] = (joined - hi.astype(F32)).astype(jnp.bfloat16)
 
+    for load in later:
+        load.wait()
+
+    path_y = ct[0, R, side[R]]
+    for c in range(R + 1, COARSE):
+        path_y = mm(path_y, ct[0, c, side[c]])
+    for s in range(X - 1):
+        sbuf[s] = mm_t(bc[0, s], path_y)
+    if R == COARSE - 3:
+        for n in range(2):
+            sbuf[X - 1 + n] = mm_t(mm(ct[0, R, n], opp[0]), ct[0, R, side[R]])
+
+
     halo_next = (
         (leaves.at[pl.ds(L0, NEAR)], leaves.at[pl.ds(0, NEAR)], nxt),
         (tiers.at[pl.ds(NODES, NODES)], tiers.at[pl.ds(0, NODES)], nxt),
@@ -247,10 +260,6 @@
 
     send_to_row(rows, 1, [p for p in places if p < half])
 
-    @pl.when(final)
-    def _():
-        send_halo(halo_next)
-
     @pl.when(first)
     def _():
         pl.semaphore_wait(state.at[1], 2 * half + one(origin))
@@ -262,29 +271,14 @@
         pl.semaphore_wait(state.at[3], 1)
 
     send_to_row(rows, 1, [p for p in places if p >= half])
-    @pl.when(jnp.logical_not(final))
-    def _():
-        send_halo(halo_next)
-
-    send_halo(halo_previous)
-
-    for load in later:
-        load.wait()
-
-    path_y = ct[0, R, side[R]]
-    for c in range(R + 1, COARSE):
-        path_y = mm(path_y, ct[0, c, side[c]])
-    for s in range(X - 1):
-        sbuf[s] = mm_t(bc[0, s], path_y)
-    if R == COARSE - 3:
-        for n in range(2):
-            sbuf[X - 1 + n] = mm_t(mm(ct[0, R, n], opp[0]), ct[0, R, side[R]])
-
+    send_halo(halo_next + halo_previous)
 
     @pl.when(first)
     def _():
         for s in range(X - 1):
             far_hi[s], far_lo[s] = split(mm(sbuf[s], (pg_hi[K:], pg_lo[K:])))
+        pl.semaphore_wait(state.at[2], 2)
+        pl.semaphore_signal(state.at[3], inc=1, device_id=mate, device_id_type=MESH)
         await_all(recv_sem.at[0], qbuf.at[pl.ds(1, W - 1)])
         total = qbuf[0]
         for n in range(1, W):
@@ -305,8 +299,6 @@
                 pltpu.make_async_remote_copy(
                     src_ref=u4buf.at[y], dst_ref=u4buf.at[y], send_sem=send_sem.at[2], recv_sem=recv_sem.at[4],
                     device_id=dev(to_y * W + j, b), device_id_type=MESH).start()
-        pl.semaphore_wait(state.at[2], 2)
-        pl.semaphore_signal(state.at[3], inc=1, device_id=mate, device_id_type=MESH)
 
     await_all(recv_sem.at[1], rows.at[pl.ds(0, W - 1)])
     tier = unpack(rows[0:W])

time: 27.2 us -> 25.5 us (0.938)
  Pallas kernels: 26.4 us -> 24.7 us
    pallas_call x1, Pallas kernels: 26.4 us -> 24.7 us  [per_device(): pl.pallas_call(functools.partial(kernel, Y, Z, X), out_shape=pltpu.VMEM(c...]
where the time goes in v2:
time: 25.5 us; the launch traced here: 25.4 us
  Pallas kernels  24.7 us (97%)
  local copies, waits for them, and re-layouts  0.62 us (2%)
    pallas_call x1, Pallas kernels, per_device(): pl.pallas_call(functools.partial(kernel, Y, Z, X), out_shape=pltpu.VMEM(c...  24.7 us
    unnamed x1, local copies, waits for them, and re-layouts  0.62 us

profile of v2, /device:TPU:1, one launch (start us, length us, event | category | flops | bytes accessed | tf_op | source)
XLA Modules:
  0.0 25.4 jit_solution(4840519671999526062)
XLA Ops:
  0.0 24.7 %shard_map.109 = f32[1,16,512]{2,1,0:T(8,128)S(1)} custom-call(s32[3,1,8]{2,1,0:T(1,128)} %bitcast.2, s32[3,1,14]{2,1,0:T(1,128)} %bitcast.3, f32[1,16,512]{2,1,0:T(8,128)} %charges_hbm.1, f32[1,8,64,64]{3,2,1,0:T(8,128)} %basis_hbm.1, f32[1,8,3,64,64]{4,3,2,1,0:T(8,128)} %near_hbm.1, f32[1,14,64,64]{3,2,1,0:T(8,128)} %transfer_hbm.1, ...), custom_call_target="tpu_custom_call" | custom-call | tf_op jit(solution)/shard_map/pallas_call | solution.py:438
  24.7 0.6 %copy.13 = f32[1,16,512]{2,1,0:T(8,128)} copy(f32[1,16,512]{2,1,0:T(8,128)S(1)} %shard_map.109) | data formatting | bytes 65536

commit v3 on v2

--- a/solution.py
+++ b/solution.py
@@ -128,8 +128,7 @@
 
     early = [(charges_hbm, charges), (basis_hbm, basis), (transfer_hbm.at[0], transfer.at[0, pl.ds(0, NODES)])]
     later = [
-        (ct_hbm, ct), (bc_hbm, bc), (opp_hbm, opp), (cc_hbm, cc), (near_hbm, near), (coupling_hbm, coupling),
-        (near_list_hbm, near_list), (coupling_list_hbm, coupling_list),
+        (cc_hbm, cc), (coupling_hbm, coupling), (near_list_hbm, near_list), (coupling_list_hbm, coupling_list),
     ]
     loads = [pltpu.make_async_copy(src, dst, load_sem.at[n]) for n, (src, dst) in enumerate(early + later)]
     early, later = loads[:len(early)], loads[len(early):]
@@ -158,6 +157,17 @@
     for load in early[:2]:
         load.wait()
 
+    @pl.when(second)
+    def _():
+        pl.semaphore_wait(barrier, 2 * half + one(final))
+        for to_z in range(half):
+            for to_k in range(2):
+                pl.semaphore_signal(state.at[1], inc=1, device_id=dev(y * W + to_z * 2 + to_k, b), device_id_type=MESH)
+
+    @pl.when(final)
+    def _():
+        pl.semaphore_signal(state.at[1], inc=1, device_id=nxt, device_id_type=MESH)
+
     dens = charges[0]
     blocks = jnp.stack([dens[:, K * l:K * (l + 1)] for l in range(L0)], axis=0)
     leaves[NEAR:NEAR + L0] = pack(blocks)
@@ -165,6 +175,8 @@
     pltpu.make_async_copy(transfer, transfer, load_sem.at[2]).wait()
     for load in later:
         load.start()
+    for src, dst in ((ct_hbm, ct), (bc_hbm, bc), (opp_hbm, opp), (near_hbm, near)):
+        pltpu.make_async_copy(src, dst, load_sem.at[7]).start()
     parts = [transfer[0, NODES + c] for c in range(R)]
     while len(parts) > 1:
         parts = [mm(*parts[n:n + 2]) if n + 1 < len(parts) else parts[n] for n in range(0, len(parts), 2)]
@@ -185,22 +197,11 @@
     tiers[NODES + 8:NODES + 12] = pack(up[1])
     tiers[NODES + 12:NODES + 14] = pack(up[2])
 
-    pl.semaphore_wait(barrier, 2 * half + one(final) + one(first) * (len(order_y) + len(order_x) - 1))
-
     @pl.when(first)
     def _():
+        pl.semaphore_wait(barrier, 2 * half - 1 + len(order_y) + len(order_x))
         for a in order_x:
             pl.semaphore_signal(state.at[0], inc=1, device_id=x_dev(a), device_id_type=MESH)
-
-    @pl.when(second)
-    def _():
-        for to_z in range(half):
-            for to_k in range(2):
-                pl.semaphore_signal(state.at[1], inc=1, device_id=dev(y * W + to_z * 2 + to_k, b), device_id_type=MESH)
-
-    @pl.when(final)
-    def _():
-        pl.semaphore_signal(state.at[1], inc=1, device_id=nxt, device_id_type=MESH)
 
     mate = dev(y * W + (Z - 1 - z) * 2 + k, b)
 
@@ -232,6 +233,7 @@
 
     for load in later:
         load.wait()
+    await_all(load_sem.at[7], coupling)
 
     path_y = ct[0, R, side[R]]
     for c in range(R + 1, COARSE):
@@ -446,7 +448,7 @@
             vm(W, 8, 128), vm(2 * W - 2, 8, 128), vm(Y, 8, 128), vm(8, 128), vm(X * Y, 8, 128), vm(4, 8, 128), vm(X + 1, K, K),
             vm(3 * NODES, 8, 128), vm(L0 + 2 * NEAR, 8, 128),
             *[pltpu.VMEM((2 * K, L0 * K), jnp.bfloat16)] * 2, *[pltpu.VMEM((X - 1, K, L0 * K), jnp.bfloat16)] * 2, vm(L0, RHS, K),
-            vm(8, 128), dma((11,)), pltpu.SemaphoreType.REGULAR((4,)), dma((4,)), dma((7,)),
+            vm(8, 128), dma((8,)), pltpu.SemaphoreType.REGULAR((4,)), dma((4,)), dma((7,)),
         ],
         compiler_params=pltpu.CompilerParams(collective_id=0, has_side_effects=True),
     )(near_at, coupling_at, *operands)

time: 25.5 us -> 25.5 us (level)
  no operation moved by 1% of the time
where the time goes in v3:
time: 25.5 us; the launch traced here: 25.3 us
  Pallas kernels  24.7 us (97%)
  local copies, waits for them, and re-layouts  0.62 us (2%)
    pallas_call x1, Pallas kernels, per_device(): pl.pallas_call(functools.partial(kernel, Y, Z, X), out_shape=pltpu.VMEM(c...  24.7 us
    unnamed x1, local copies, waits for them, and re-layouts  0.62 us

profile of v3, /device:TPU:1, one launch (start us, length us, event | category | flops | bytes accessed | tf_op | source)
XLA Modules:
  0.0 25.3 jit_solution(2283266518102292949)
XLA Ops:
  0.0 24.7 %shard_map.109 = f32[1,16,512]{2,1,0:T(8,128)S(1)} custom-call(s32[3,1,8]{2,1,0:T(1,128)} %bitcast.2, s32[3,1,14]{2,1,0:T(1,128)} %bitcast.3, f32[1,16,512]{2,1,0:T(8,128)} %charges_hbm.1, f32[1,8,64,64]{3,2,1,0:T(8,128)} %basis_hbm.1, f32[1,8,3,64,64]{4,3,2,1,0:T(8,128)} %near_hbm.1, f32[1,14,64,64]{3,2,1,0:T(8,128)} %transfer_hbm.1, ...), custom_call_target="tpu_custom_call" | custom-call | tf_op jit(solution)/shard_map/pallas_call | solution.py:440
  24.7 0.6 %copy.13 = f32[1,16,512]{2,1,0:T(8,128)} copy(f32[1,16,512]{2,1,0:T(8,128)S(1)} %shard_map.109) | data formatting | bytes 65536
